TPU v7x, 32 devices: a whole 2x2x4 slice. The times are simulated.
32 devices in a mesh: groups: 2 (over x), tensor: 8 (over z, y), batch: 2 (over core).
Axes of the slice: x: 2, y: 2, z: 4, core: 2. Of those that a mesh axis runs over, the one named last changes fastest.
Arguments:
- hidden: bfloat16 [256, 2, 8192], P(('groups', 'tensor', 'batch')), parts along dimension 0, may hold values from -6 to 6
- wq: bfloat16 [8192, 8192], P(None, 'tensor'), may hold values from -0.0625 to 0.0625
- wkv: bfloat16 [8192, 2048], P(None, 'tensor'), may hold values from -0.0625 to 0.0625
- cache_pool: bfloat16 [512, 128, 2048], P(('groups', 'tensor', 'batch')), parts along dimension 0, may hold values from -240 to 240
- page_table: int32 [256, 2], P(('groups', 'tensor', 'batch')), parts along dimension 0, may hold values from 0 to 15, as said below
- ctx_len: int32 [256], P(('groups', 'tensor', 'batch')), parts along dimension 0, may hold values from 1 to 256
- prompt_slot: int32 [32], P(('groups', 'tensor', 'batch')), parts along dimension 0, may hold values from 0 to 7
- prompt_kv: bfloat16 [32, 128, 2048], P(('groups', 'batch'), None, 'tensor'), parts along dimension 0, may hold values from -6 to 6
Outputs:
- attended: bfloat16 [256, 2, 8192], P(('groups', 'tensor', 'batch')), parts along dimension 0
There are 2 independent parts, one for each index of `groups`. A program takes and returns all parts, laid end to end along the dimension named above; an argument that names none is the same for every part. Nothing has to cross between parts.
Inputs may be any that keep to these rules, and one draw needn't show every extreme that they name: `page_table`: within each block of 8 sequences the entries name each of that block's 16 local pages exactly once; entry p holds the sequence's tokens p * 128 to (p + 1) * 128 - 1.
All inputs are finite; a program needn't handle non-finite values.
Results may differ from a plain program's by a relative error of at most 0.012.
Values may be sent and summed in bfloat16 or wider, within the bound.
A program may use at most 128 MiB of HBM per device.

v0:
```python
import functools

import jax
import jax.numpy as jnp
from jax import lax
from jax.experimental import pallas as pl
from jax.experimental.pallas import tpu as pltpu
from jax.sharding import PartitionSpec as P

QUERY_HEADS = 64
KEY_VALUE_HEADS = 8
HEAD_SIZE = 128
GROUP = QUERY_HEADS // KEY_VALUE_HEADS
MESH = pl.DeviceIdType.MESH
NEG = -1e30
UNROLL = 2


def dot_t(a, b):
    return lax.dot_general(a, b, (((1,), (1,)), ((), ())), preferred_element_type=jnp.float32)


def attend_kernel(
    seqs, pages, table, lens, slot, *refs
):
    page_refs = refs[:pages]
    q_ref, kv_ref, prompt_ref, out_ref, qp, op = refs[pages:]
    s = pl.program_id(0)
    rows = seqs * 2
    block = 2 * GROUP
    total = rows * GROUP
    kv_half = KEY_VALUE_HEADS * HEAD_SIZE

    def perm(transposed):
        r = lax.broadcasted_iota(jnp.int32, (total, total), 1 if transposed else 0)
        c = lax.broadcasted_iota(jnp.int32, (total, total), 0 if transposed else 1)
        seq, rest = r // block, r % block
        source = (rest % GROUP) * rows + seq * 2 + rest // GROUP
        return jnp.where(c == source, 1.0, 0.0).astype(jnp.bfloat16)

    @pl.when(s == 0)
    def _():
        p = perm(False)
        for h in range(KEY_VALUE_HEADS):
            tiles = [
                q_ref[:, (h * GROUP + g) * HEAD_SIZE : (h * GROUP + g + 1) * HEAD_SIZE]
                for g in range(GROUP)
            ]
            stacked = jnp.concatenate(tiles, axis=0)
            qp[h] = jnp.dot(p, stacked, preferred_element_type=jnp.float32).astype(jnp.bfloat16)

    page_rows = page_refs[0].shape[1]
    length = lens[s]
    lane = lax.broadcasted_iota(jnp.int32, (block, page_rows), 1)
    new_col = lax.broadcasted_iota(jnp.int32, (block, rows), 1)
    new_row = lax.broadcasted_iota(jnp.int32, (block, rows), 0)
    new_live = (new_col // 2 == s) & (new_col % 2 <= new_row // GROUP)
    here = pl.ds(pl.multiple_of(s * block, block), block)
    scale = HEAD_SIZE ** (-0.5)

    def heads(with_prompt):
        for h in range(KEY_VALUE_HEADS):
            kc = slice(h * HEAD_SIZE, (h + 1) * HEAD_SIZE)
            vc = slice(kv_half + h * HEAD_SIZE, kv_half + (h + 1) * HEAD_SIZE)
            qh = qp[h, here, :]
            parts = []
            for p in range(pages):
                sc = dot_t(qh, page_refs[p][0, :, kc]) * scale
                parts.append((jnp.where(lane + p * page_rows < length, sc, NEG), page_refs[p][0, :, vc]))
            sc = dot_t(qh, kv_ref[:, kc]) * scale
            parts.append((jnp.where(new_live, sc, NEG), kv_ref[:, vc]))
            if with_prompt:
                parts.append((dot_t(qh, prompt_ref[:, kc]) * scale, prompt_ref[:, vc]))
            top = functools.reduce(
                jnp.maximum, [jnp.max(sc, axis=-1, keepdims=True) for sc, _ in parts]
            )
            expo = [jnp.exp(sc - top) for sc, _ in parts]
            norm = functools.reduce(
                jnp.add, [jnp.sum(e, axis=-1, keepdims=True) for e in expo]
            )
            acc = functools.reduce(
                jnp.add,
                [
                    jnp.dot(e.astype(jnp.bfloat16), v, preferred_element_type=jnp.float32)
                    for e, (_, v) in zip(expo, parts)
                ],
            )
            op[h, here, :] = (acc / norm).astype(jnp.bfloat16)

    mine = s == slot[0]

    @pl.when(mine)
    def _():
        heads(True)

    @pl.when(jnp.logical_not(mine))
    def _():
        heads(False)

    @pl.when(s == seqs - 1)
    def _():
        p = perm(True)
        for h in range(KEY_VALUE_HEADS):
            back = jnp.dot(p, op[h], preferred_element_type=jnp.float32).astype(jnp.bfloat16)
            for g in range(GROUP):
                out_ref[:, (h * GROUP + g) * HEAD_SIZE : (h * GROUP + g + 1) * HEAD_SIZE] = back[
                    g * rows : (g + 1) * rows, :
                ]


def attend(query, keyval, prompt, pool, table, lens, slot):
    seqs, pages = table.shape
    page_rows, kv_cols = pool.shape[1:]
    rows = query.shape[0]

    def page_spec(p):
        return pl.BlockSpec((1, page_rows, kv_cols), lambda s, t, l, sl: (t[s * pages + p], 0, 0))

    def whole(x):
        return pl.BlockSpec(x.shape, lambda s, t, l, sl: (0,) * x.ndim)

    total = rows * GROUP
    return pl.pallas_call(
        functools.partial(attend_kernel, seqs, pages),
        grid_spec=pltpu.PrefetchScalarGridSpec(
            num_scalar_prefetch=3,
            grid=(seqs,),
            in_specs=[page_spec(p) for p in range(pages)] + [whole(query), whole(keyval), whole(prompt)],
            out_specs=pl.BlockSpec(query.shape, lambda s, t, l, sl: (0, 0)),
            scratch_shapes=[
                pltpu.VMEM((KEY_VALUE_HEADS, total, HEAD_SIZE), jnp.bfloat16),
                pltpu.VMEM((KEY_VALUE_HEADS, total, HEAD_SIZE), jnp.bfloat16),
            ],
        ),
        out_shape=jax.ShapeDtypeStruct(query.shape, jnp.bfloat16),
        compiler_params=pltpu.CompilerParams(dimension_semantics=("arbitrary",)),
        name="attend",
    )(table.reshape(-1), lens, slot, *([pool] * pages), query, keyval, prompt)


def attend_resident(table, lens, slot, pool_v, q_out, kv_out, prompt_out, qbd, op, out, after):
    seqs = lens.shape[0]
    pages = table.shape[0] // seqs
    rows = seqs * 2
    block = 2 * GROUP
    total = rows * GROUP
    kv_half = KEY_VALUE_HEADS * HEAD_SIZE
    page_rows = pool_v.shape[1]
    lanes = KEY_VALUE_HEADS * block
    scale = HEAD_SIZE ** (-0.5)

    def perm(transposed):
        r = lax.broadcasted_iota(jnp.int32, (total, total), 1 if transposed else 0)
        c = lax.broadcasted_iota(jnp.int32, (total, total), 0 if transposed else 1)
        seq, rest = r // block, r % block
        source = (rest % GROUP) * rows + seq * 2 + rest // GROUP
        return jnp.where(c == source, 1.0, 0.0).astype(jnp.bfloat16)

    p = perm(False)
    for h in range(KEY_VALUE_HEADS):
        tiles = [
            q_out[:, (h * GROUP + g) * HEAD_SIZE : (h * GROUP + g + 1) * HEAD_SIZE]
            for g in range(GROUP)
        ]
        ordered = jnp.dot(
            p, jnp.concatenate(tiles, axis=0), preferred_element_type=jnp.float32
        ).astype(jnp.bfloat16)
        for s in range(seqs):
            qbd[s, h * block : (h + 1) * block, h * HEAD_SIZE : (h + 1) * HEAD_SIZE] = ordered[
                s * block : (s + 1) * block, :
            ]

    key = lax.broadcasted_iota(jnp.int32, (page_rows, lanes), 0)
    new_key = lax.broadcasted_iota(jnp.int32, (rows, lanes), 0)
    new_pos = lax.broadcasted_iota(jnp.int32, (rows, lanes), 1) // GROUP % 2

    def one(s, with_prompt):
        q = qbd[s]
        where_pages = [table[s * pages + p] for p in range(pages)]
        parts = []
        for p in range(pages):
            sc = dot_t(pool_v[where_pages[p], :, :kv_half], q) * scale
            parts.append(jnp.where(key + p * page_rows < lens[s], sc, NEG))
        if with_prompt:
            parts.append(dot_t(prompt_out[:, :kv_half], q) * scale)
        sc = dot_t(kv_out[:, :kv_half], q) * scale
        parts.append(jnp.where((new_key // 2 == s) & (new_key % 2 <= new_pos), sc, NEG))
        top = functools.reduce(jnp.maximum, [jnp.max(x, axis=0, keepdims=True) for x in parts])
        expo = [jnp.exp(x - top) for x in parts]
        norm = functools.reduce(jnp.add, [jnp.sum(e, axis=0, keepdims=True) for e in expo])
        weights = [jnp.transpose(e / norm).astype(jnp.bfloat16) for e in expo]
        wide = jnp.concatenate(weights[:pages], axis=1)
        outs = []
        for h in range(KEY_VALUE_HEADS):
            vc = slice(kv_half + h * HEAD_SIZE, kv_half + (h + 1) * HEAD_SIZE)
            mine = slice(h * block, (h + 1) * block)
            v = jnp.concatenate([pool_v[w, :, vc] for w in where_pages], axis=0)
            acc = jnp.dot(wide[mine], v, preferred_element_type=jnp.float32)
            acc += jnp.dot(weights[-1][mine], kv_out[:, vc], preferred_element_type=jnp.float32)
            if with_prompt:
                acc += jnp.dot(weights[pages][mine], prompt_out[:, vc], preferred_element_type=jnp.float32)
            outs.append(acc.astype(jnp.bfloat16))
        return outs

    def several(k, carry):
        for u in range(UNROLL):
            s = k * UNROLL + u
            for h, o in enumerate(one(s, False)):
                op[h, pl.ds(pl.multiple_of(s * block, block), block), :] = o
        return carry

    lax.fori_loop(0, seqs // UNROLL, several, 0)
    after()
    chosen = slot[0]
    continued = one(chosen, True)
    row_seq = lax.broadcasted_iota(jnp.int32, (total, HEAD_SIZE), 0) // block
    p = perm(True)
    for h in range(KEY_VALUE_HEADS):
        spread = jnp.concatenate([continued[h]] * seqs, axis=0)
        mixed = jnp.where(row_seq == chosen, spread, op[h])
        back = jnp.dot(p, mixed, preferred_element_type=jnp.float32).astype(jnp.bfloat16)
        for g in range(GROUP):
            out[:, (h * GROUP + g) * HEAD_SIZE : (h * GROUP + g + 1) * HEAD_SIZE] = back[
                g * rows : (g + 1) * rows, :
            ]


def relay_kernel(
    n, chunks, table, lens, slot, hidden, wq, wkv, prompt, pool, attended,
    q_out, kv_out, prompt_out, prompt_v, pool_v, qbd, op,
    gath, wq_v, wkv_v, acc_q, acc_kv, stage_q, stage_kv,
    right_send, right_recv, left_send, left_recv,
    q_send, q_recv, kv_send, kv_recv, p_send, p_recv, w_sem, local_sem,
):
    me = lax.axis_index("tensor")
    rows, depth = hidden.shape
    width = depth // chunks
    q_cols, kv_cols = wq.shape[1], wkv.shape[1]
    half = n // 2
    pos = jnp.where(me % 2 == 0, me // 2, n - 1 - me // 2)

    def at(position):
        p = lax.rem(position + 2 * n, n)
        return jnp.where(p < half, 2 * p, 2 * (n - 1 - p) + 1)

    def slot_of(direction, hop):
        return 0 if hop == 0 else n - 1 if hop == half else 2 * hop - 1 + direction

    def rows_of(k, count=1):
        return pl.ds(k * rows, count * rows)

    own = pltpu.make_async_copy(hidden, gath.at[rows_of(0), :], local_sem.at[0])
    own.start()
    weights = []
    for c in range(chunks):
        k = pl.ds(c * width, width)
        pair = (
            pltpu.make_async_copy(wq.at[k, :], wq_v.at[k, :], w_sem.at[0, c]),
            pltpu.make_async_copy(wkv.at[k, :], wkv_v.at[k, :], w_sem.at[1, c]),
        )
        for copy in pair:
            copy.start()
        weights.append(pair)
    load_prompt = pltpu.make_async_copy(prompt, prompt_v, local_sem.at[4])
    load_prompt.start()
    load_pool = pltpu.make_async_copy(pool, pool_v, local_sem.at[5])
    load_pool.start()

    barrier = pltpu.get_barrier_semaphore()
    for d in range(1, n):
        pl.semaphore_signal(
            barrier, inc=1, device_id={"tensor": lax.rem(me + d, n)}, device_id_type=MESH
        )
    pl.semaphore_wait(barrier, n - 1)

    def goes(direction, hop, c):
        return hop < half or (hop == half and c % 2 == direction)

    def ring_copy(direction, hop, c):
        sign = 1 if direction == 0 else -1
        cols = pl.ds(c * width, width)
        send, recv = (right_send, right_recv) if direction == 0 else (left_send, left_recv)
        return pltpu.make_async_remote_copy(
            src_ref=gath.at[rows_of(slot_of(direction, hop - 1)), cols],
            dst_ref=gath.at[rows_of(slot_of(direction, hop)), cols],
            send_sem=send.at[hop - 1, c],
            recv_sem=recv.at[hop - 1, c],
            device_id={"tensor": at(pos + sign)},
            device_id_type=MESH,
        )

    started = {}

    def launch(hop, c):
        for direction in (0, 1):
            if goes(direction, hop, c):
                copy = ring_copy(direction, hop, c)
                copy.start()
                started[direction, hop, c] = copy

    def arrive(hop, c):
        for direction in (0, 1):
            if goes(direction, hop, c):
                started[direction, hop, c].wait_recv()

    def multiply(first, count, c):
        if first == 0:
            for copy in weights[c]:
                copy.wait()
        taken = slice(first * rows, (first + count) * rows)
        x = gath[taken, c * width : (c + 1) * width]
        for w, acc in ((wq_v, acc_q), (wkv_v, acc_kv)):
            part = jnp.dot(x, w[c * width : (c + 1) * width, :], preferred_element_type=jnp.float32)
            if c == 0:
                acc[taken, :] = part
            else:
                acc[taken, :] += part

    results = []

    def hand_out(first, count):
        taken = slice(first * rows, (first + count) * rows)
        stage_q[taken, :] = acc_q[taken, :].astype(jnp.bfloat16)
        stage_kv[taken, :] = acc_kv[taken, :].astype(jnp.bfloat16)
        for k in range(max(first, 1), first + count):
            hops = (k + 1) // 2
            t = at(pos - hops if k % 2 == 1 else pos + hops)
            for stage, out, cols, send, recv in (
                (stage_q, q_out, q_cols, q_send, q_recv),
                (stage_kv, kv_out, kv_cols, kv_send, kv_recv),
            ):
                copy = pltpu.make_async_remote_copy(
                    src_ref=stage.at[rows_of(k), :],
                    dst_ref=out.at[:, pl.ds(pl.multiple_of(me * cols, cols), cols)],
                    send_sem=send.at[k],
                    recv_sem=recv.at[k],
                    device_id={"tensor": t},
                    device_id_type=MESH,
                )
                copy.start()
                results.append(copy)

    own.wait()
    for c in range(chunks):
        launch(1, c)
    qbd[...] = jnp.zeros_like(qbd)
    load_prompt.wait()
    for hop in range(1, half - 1):
        for c in range(chunks):
            arrive(hop, c)
            launch(hop + 1, c)
    early = 2 * (half - 2) + 1
    for c in range(chunks):
        multiply(0, early, c)
        arrive(half - 1, c)
        launch(half, c)
    hand_out(0, early)
    for c in range(chunks):
        arrive(half, c)
        multiply(early, n - early, c)
    hand_out(early, n - early)
    prompts = []
    for d in range(1, n):
        t = lax.rem(me + d, n)
        copy = pltpu.make_async_remote_copy(
            src_ref=prompt_v.at[t],
            dst_ref=prompt_out.at[:, pl.ds(pl.multiple_of(me * kv_cols, kv_cols), kv_cols)],
            send_sem=p_send.at[d],
            recv_sem=p_recv.at[d],
            device_id={"tensor": t},
            device_id_type=MESH,
        )
        prompts.append(copy)
    for copy in prompts:
        copy.start()
    mine = []
    for k, (source, out, cols) in enumerate(
        (
            (stage_q.at[rows_of(0), :], q_out, q_cols),
            (stage_kv.at[rows_of(0), :], kv_out, kv_cols),
            (prompt_v.at[me], prompt_out, kv_cols),
        )
    ):
        copy = pltpu.make_async_copy(
            source, out.at[:, pl.ds(pl.multiple_of(me * cols, cols), cols)], local_sem.at[1 + k]
        )
        copy.start()
        mine.append(copy)
    for copy in results + mine:
        copy.wait()
    load_pool.wait()

    def after():
        for copy in prompts:
            copy.wait()

    attend_resident(
        table, lens, slot, pool_v, q_out, kv_out, prompt_out, qbd, op, attended, after
    )
    for copy in started.values():
        copy.wait_send()


def relay(hidden, wq, wkv, prompt, pool, table, lens, slot, n):
    rows, depth = hidden.shape
    q_cols, kv_cols = wq.shape[1], wkv.shape[1]
    chunks = 8
    half = n // 2
    vmem = pl.BlockSpec(memory_space=pltpu.VMEM)
    hbm = pl.BlockSpec(memory_space=pl.ANY)
    dma = pltpu.SemaphoreType.DMA
    plen = prompt.shape[1]
    seqs = rows // 2
    smem = pl.BlockSpec(memory_space=pltpu.SMEM)
    return pl.pallas_call(
        functools.partial(relay_kernel, n, chunks),
        out_shape=jax.ShapeDtypeStruct((rows, q_cols * n), jnp.bfloat16),
        in_specs=[smem, smem, smem, hbm, hbm, hbm, hbm, hbm],
        out_specs=vmem,
        scratch_shapes=[
            pltpu.VMEM((rows, q_cols * n), jnp.bfloat16),
            pltpu.VMEM((rows, kv_cols * n), jnp.bfloat16),
            pltpu.VMEM((plen, kv_cols * n), jnp.bfloat16),
            pltpu.VMEM(prompt.shape, jnp.bfloat16),
            pltpu.VMEM(pool.shape, jnp.bfloat16),
            pltpu.VMEM((seqs, KEY_VALUE_HEADS * 2 * GROUP, KEY_VALUE_HEADS * HEAD_SIZE), jnp.bfloat16),
            pltpu.VMEM((KEY_VALUE_HEADS, rows * GROUP, HEAD_SIZE), jnp.bfloat16),
            pltpu.VMEM((n * rows, depth), jnp.bfloat16),
            pltpu.VMEM((depth, q_cols), jnp.bfloat16),
            pltpu.VMEM((depth, kv_cols), jnp.bfloat16),
            pltpu.VMEM((n * rows, q_cols), jnp.float32),
            pltpu.VMEM((n * rows, kv_cols), jnp.float32),
            pltpu.VMEM((n * rows, q_cols), jnp.bfloat16),
            pltpu.VMEM((n * rows, kv_cols), jnp.bfloat16),
            dma((half, chunks)),
            dma((half, chunks)),
            dma((half, chunks)),
            dma((half, chunks)),
            dma((n,)),
            dma((n,)),
            dma((n,)),
            dma((n,)),
            dma((n,)),
            dma((n,)),
            dma((2, chunks)),
            dma((6,)),
        ],
        compiler_params=pltpu.CompilerParams(
            collective_id=0, has_side_effects=True, vmem_limit_bytes=60 << 20
        ),
        name="relay",
    )(table.reshape(-1), lens, slot, hidden, wq, wkv, prompt, pool)


def exchange(hidden, wq, wkv, prompt_kv):
    prompt = lax.all_to_all(prompt_kv, "tensor", split_axis=0, concat_axis=2, tiled=True)[0]
    gathered = lax.all_gather(hidden, "tensor", axis=0, tiled=True)
    outs = []
    for w in (wq, wkv):
        part = jnp.dot(gathered, w, preferred_element_type=jnp.float32).astype(jnp.bfloat16)
        outs.append(lax.all_to_all(part, "tensor", split_axis=0, concat_axis=1, tiled=True))
    return outs[0], outs[1], prompt


def per_device(n, hidden, wq, wkv, cache_pool, page_table, ctx_len, prompt_slot, prompt_kv):
    seqs = hidden.shape[0]
    flat = hidden.reshape(seqs * 2, hidden.shape[2])
    aligned = wq.shape[1] % 128 == 0 and wkv.shape[1] % 128 == 0
    if aligned and n % 2 == 0 and n > 4 and flat.shape[0] % 16 == 0 and prompt_kv.shape[0] == n:
        out = relay(flat, wq, wkv, prompt_kv, cache_pool, page_table, ctx_len, prompt_slot, n)
    else:
        query, keyval, prompt = exchange(flat, wq, wkv, prompt_kv)
        out = attend(query, keyval, prompt, cache_pool, page_table, ctx_len, prompt_slot)
    return out.reshape(seqs, 2, out.shape[1])


def solution(mesh):
    placed = (
        P(("groups", "tensor", "batch"), None, None),
        P(None, "tensor"),
        P(None, "tensor"),
        P(("groups", "tensor", "batch"), None, None),
        P(("groups", "tensor", "batch"), None),
        P(("groups", "tensor", "batch")),
        P(("groups", "tensor", "batch")),
        P(("groups", "batch"), None, "tensor"),
    )
    return jax.shard_map(
        functools.partial(per_device, mesh.shape["tensor"]),
        mesh=mesh,
        in_specs=placed,
        out_specs=P(("groups", "tensor", "batch"), None, None),
        check_vma=False,
    )
```

profile of v0, /device:TPU:0, one launch (start us, length us, event | category | flops | bytes accessed | tf_op | source)
XLA Modules:
  0.0 59.9 jit_solution(13101839723709422117)
XLA Ops:
  0.7 0.8 %copy.10 = s32[8,2]{1,0:T(8,128)S(1)} copy(s32[8,2]{0,1:T(2,128)} %param.12) | data formatting | bytes 128 | tf_op args[4]
  1.4 0.7 %reshape.9.table = s32[16]{0:T(128)} reshape(s32[8,2]{1,0:T(8,128)S(1)} %copy.10) | data formatting | bytes 128 | tf_op jit(solution)/shard_map/reshape | solution.py:452
  2.1 1.8 %reshape.10.hidden = bf16[16,8192]{1,0:T(8,128)(2,1)} reshape(bf16[8,2,8192]{2,1,0:T(2,128)(2,1)} %param.8) | data formatting | bytes 524288 | tf_op jit(solution)/shard_map/reshape | solution.py:467
  3.8 54.2 %relay.1 = bf16[16,8192]{1,0:T(8,128)(2,1)} custom-call(s32[16]{0:T(128)} %reshape.9.table, s32[8]{0:T(128)} %lens.1, s32[1]{0:T(128)S(6)} %copy.11.slot, bf16[16,8192]{1,0:T(8,128)(2,1)} %reshape.10.hidden, bf16[8192,1024]{1,0:T(8,128)(2,1)} %wq.1, bf16[8192,256]{1,0:T(8,128)(2,1)} %wkv.1, bf16[8,128,256]{2,1,0:T(8,128)(2,1)} %prompt.1, ...), custom_call_target="tpu_custom_call" | custom-call | tf_op jit(solution)/shard_map/relay/pallas_call | solution.py:415
  58.0 1.8 %reshape.11 = bf16[8,2,8192]{2,1,0:T(2,128)(2,1)} reshape(bf16[16,8192]{1,0:T(8,128)(2,1)} %relay.1) | data formatting | bytes 524288 | tf_op jit(solution)/shard_map/reshape | solution.py:474
where the time goes:
time: 60.1 us; the launch traced here: 59.9 us
  Pallas kernels  54.2 us (90%)
  local copies, waits for them, and re-layouts  4.99 us (8%)
  between operations  0.66 us (1%)
    pallas_call x1, Pallas kernels, relay(): pl.pallas_call(functools.partial(relay_kernel, n, chunks), out_shape=jax....  54.2 us
    reshape x1, local copies, waits for them, and re-layouts, per_device(): return out.reshape(seqs, 2, out.shape[1])  1.83 us
    reshape x1, local copies, waits for them, and re-layouts, per_device(): flat = hidden.reshape(seqs * 2, hidden.shape[2])  1.75 us

commit v1 on v0

--- a/solution.py
+++ b/solution.py
@@ -140,7 +140,7 @@
 
 def attend_resident(table, lens, slot, pool_v, q_out, kv_out, prompt_out, qbd, op, out, after):
     seqs = lens.shape[0]
-    pages = table.shape[0] // seqs
+    pages = table.shape[0]
     rows = seqs * 2
     block = 2 * GROUP
     total = rows * GROUP
@@ -176,7 +176,7 @@
 
     def one(s, with_prompt):
         q = qbd[s]
-        where_pages = [table[s * pages + p] for p in range(pages)]
+        where_pages = [table[p, s] for p in range(pages)]
         parts = []
         for p in range(pages):
             sc = dot_t(pool_v[where_pages[p], :, :kv_half], q) * scale
@@ -226,14 +226,15 @@
 
 
 def relay_kernel(
-    n, chunks, table, lens, slot, hidden, wq, wkv, prompt, pool, attended,
+    n, chunks, table_h, lens_h, slot_h, hidden, wq, wkv, prompt, pool, attended,
+    table, lens, slot, hid_v,
     q_out, kv_out, prompt_out, prompt_v, pool_v, qbd, op,
     gath, wq_v, wkv_v, acc_q, acc_kv, stage_q, stage_kv,
     right_send, right_recv, left_send, left_recv,
     q_send, q_recv, kv_send, kv_recv, p_send, p_recv, w_sem, local_sem,
 ):
     me = lax.axis_index("tensor")
-    rows, depth = hidden.shape
+    rows, depth = attended.shape[0], hidden.shape[2]
     width = depth // chunks
     q_cols, kv_cols = wq.shape[1], wkv.shape[1]
     half = n // 2
@@ -249,8 +250,18 @@
     def rows_of(k, count=1):
         return pl.ds(k * rows, count * rows)
 
-    own = pltpu.make_async_copy(hidden, gath.at[rows_of(0), :], local_sem.at[0])
+    barrier = pltpu.get_barrier_semaphore()
+    for sign in (-1, 1):
+        pl.semaphore_signal(
+            barrier, inc=1, device_id={"tensor": at(pos + sign)}, device_id_type=MESH
+        )
+    own = pltpu.make_async_copy(hidden, hid_v, local_sem.at[0])
     own.start()
+    scalars = []
+    for k, (src, dst) in enumerate(((table_h, table), (lens_h, lens), (slot_h, slot))):
+        copy = pltpu.make_async_copy(src, dst, local_sem.at[1 + k])
+        copy.start()
+        scalars.append(copy)
     weights = []
     for c in range(chunks):
         k = pl.ds(c * width, width)
@@ -265,13 +276,6 @@
     load_prompt.start()
     load_pool = pltpu.make_async_copy(pool, pool_v, local_sem.at[5])
     load_pool.start()
-
-    barrier = pltpu.get_barrier_semaphore()
-    for d in range(1, n):
-        pl.semaphore_signal(
-            barrier, inc=1, device_id={"tensor": lax.rem(me + d, n)}, device_id_type=MESH
-        )
-    pl.semaphore_wait(barrier, n - 1)
 
     def goes(direction, hop, c):
         return hop < half or (hop == half and c % 2 == direction)
@@ -341,6 +345,10 @@
                 results.append(copy)
 
     own.wait()
+    for c in range(chunks):
+        cols = slice(c * width, (c + 1) * width)
+        gath[rows_of(0), cols] = hid_v[:, :, cols].reshape(rows, width)
+    pl.semaphore_wait(barrier, 2)
     for c in range(chunks):
         launch(1, c)
     qbd[...] = jnp.zeros_like(qbd)
@@ -373,20 +381,15 @@
         prompts.append(copy)
     for copy in prompts:
         copy.start()
-    mine = []
-    for k, (source, out, cols) in enumerate(
-        (
-            (stage_q.at[rows_of(0), :], q_out, q_cols),
-            (stage_kv.at[rows_of(0), :], kv_out, kv_cols),
-            (prompt_v.at[me], prompt_out, kv_cols),
-        )
+    for source, out, cols in (
+        (stage_q[0:rows, :], q_out, q_cols),
+        (stage_kv[0:rows, :], kv_out, kv_cols),
+        (prompt_v[me], prompt_out, kv_cols),
     ):
-        copy = pltpu.make_async_copy(
-            source, out.at[:, pl.ds(pl.multiple_of(me * cols, cols), cols)], local_sem.at[1 + k]
-        )
-        copy.start()
-        mine.append(copy)
-    for copy in results + mine:
+        out[:, pl.ds(pl.multiple_of(me * cols, cols), cols)] = source
+    for copy in results:
+        copy.wait()
+    for copy in scalars:
         copy.wait()
     load_pool.wait()
 
@@ -402,22 +405,26 @@
 
 
 def relay(hidden, wq, wkv, prompt, pool, table, lens, slot, n):
-    rows, depth = hidden.shape
+    seqs, per, depth = hidden.shape
+    rows = seqs * per
     q_cols, kv_cols = wq.shape[1], wkv.shape[1]
     chunks = 8
     half = n // 2
     vmem = pl.BlockSpec(memory_space=pltpu.VMEM)
-    hbm = pl.BlockSpec(memory_space=pl.ANY)
+    hbm = pl.BlockSpec(memory_space=pltpu.HBM)
     dma = pltpu.SemaphoreType.DMA
     plen = prompt.shape[1]
-    seqs = rows // 2
-    smem = pl.BlockSpec(memory_space=pltpu.SMEM)
+    table = table.T
     return pl.pallas_call(
         functools.partial(relay_kernel, n, chunks),
         out_shape=jax.ShapeDtypeStruct((rows, q_cols * n), jnp.bfloat16),
-        in_specs=[smem, smem, smem, hbm, hbm, hbm, hbm, hbm],
+        in_specs=[hbm] * 8,
         out_specs=vmem,
         scratch_shapes=[
+            pltpu.SMEM(table.shape, table.dtype),
+            pltpu.SMEM(lens.shape, lens.dtype),
+            pltpu.SMEM(slot.shape, slot.dtype),
+            pltpu.VMEM(hidden.shape, jnp.bfloat16),
             pltpu.VMEM((rows, q_cols * n), jnp.bfloat16),
             pltpu.VMEM((rows, kv_cols * n), jnp.bfloat16),
             pltpu.VMEM((plen, kv_cols * n), jnp.bfloat16),
@@ -449,7 +456,7 @@
             collective_id=0, has_side_effects=True, vmem_limit_bytes=60 << 20
         ),
         name="relay",
-    )(table.reshape(-1), lens, slot, hidden, wq, wkv, prompt, pool)
+    )(table, lens, slot, hidden, wq, wkv, prompt, pool)
 
 
 def exchange(hidden, wq, wkv, prompt_kv):
@@ -467,7 +474,7 @@
     flat = hidden.reshape(seqs * 2, hidden.shape[2])
     aligned = wq.shape[1] % 128 == 0 and wkv.shape[1] % 128 == 0
     if aligned and n % 2 == 0 and n > 4 and flat.shape[0] % 16 == 0 and prompt_kv.shape[0] == n:
-        out = relay(flat, wq, wkv, prompt_kv, cache_pool, page_table, ctx_len, prompt_slot, n)
+        out = relay(hidden, wq, wkv, prompt_kv, cache_pool, page_table, ctx_len, prompt_slot, n)
     else:
         query, keyval, prompt = exchange(flat, wq, wkv, prompt_kv)
         out = attend(query, keyval, prompt, cache_pool, page_table, ctx_len, prompt_slot)

time: 60.1 us -> 55 us (0.915)
  local copies, waits for them, and re-layouts: 4.99 us -> 1.83 us
  Pallas kernels: 54.2 us -> 52.3 us
    reshape x2 -> x0, local copies, waits for them, and re-layouts: 2.4 us -> none  [the longest x1 1.75 us: per_device(): flat = hidden.reshape(seqs * 2, hidden.shape[2])]
    pallas_call x1, Pallas kernels: 54.2 us -> 52.3 us  [relay(): pl.pallas_call(functools.partial(relay_kernel, n, chunks), out_shape=jax....]
    unnamed x1 -> x0, local copies, waits for them, and re-layouts: 0.75 us -> none
where the time goes in v1:
time: 55 us; the launch traced here: 54.8 us
  Pallas kernels  52.3 us (95%)
  local copies, waits for them, and re-layouts  1.83 us (3%)
  between operations  0.66 us (1%)
    pallas_call x1, Pallas kernels, relay(): pl.pallas_call(functools.partial(relay_kernel, n, chunks), out_shape=jax....  52.3 us
    reshape x1, local copies, waits for them, and re-layouts, per_device(): return out.reshape(seqs, 2, out.shape[1])  1.83 us

profile of v1, /device:TPU:0, one launch (start us, length us, event | category | flops | bytes accessed | tf_op | source)
XLA Modules:
  0.0 54.8 jit_solution(18123192595127575253)
XLA Ops:
  0.7 52.3 %relay.1 = bf16[16,8192]{1,0:T(8,128)(2,1)} custom-call(s32[2,8]{1,0:T(2,128)} %bitcast.1, s32[8]{0:T(128)} %lens_h.1, s32[1]{0:T(128)S(6)} %copy.9.slot_h, bf16[8,2,8192]{2,1,0:T(2,128)(2,1)} %hidden.1, bf16[8192,1024]{1,0:T(8,128)(2,1)} %wq.1, bf16[8192,256]{1,0:T(8,128)(2,1)} %wkv.1, bf16[8,128,256]{2,1,0:T(8,128)(2,1)} %prompt.1, bf16[16,128,2048]{2,1,0:T(8,128)(2,1)} %pool.1), custom_call_target="tpu_custom_call" | custom-call | tf_op jit(solution)/shard_map/relay/pallas_call | solution.py:418
  53.0 1.8 %reshape.3 = bf16[8,2,8192]{2,1,0:T(2,128)(2,1)} reshape(bf16[16,8192]{1,0:T(8,128)(2,1)} %relay.1) | data formatting | bytes 524288 | tf_op jit(solution)/shard_map/reshape | solution.py:481

commit v2 on v1

--- a/solution.py
+++ b/solution.py
@@ -230,31 +230,48 @@
     table, lens, slot, hid_v,
     q_out, kv_out, prompt_out, prompt_v, pool_v, qbd, op,
     gath, wq_v, wkv_v, acc_q, acc_kv, stage_q, stage_kv,
-    right_send, right_recv, left_send, left_recv,
+    own_send, z_send, z_recv, y_send, y_recv,
     q_send, q_recv, kv_send, kv_recv, p_send, p_recv, w_sem, local_sem,
 ):
     me = lax.axis_index("tensor")
     rows, depth = attended.shape[0], hidden.shape[2]
     width = depth // chunks
     q_cols, kv_cols = wq.shape[1], wkv.shape[1]
-    half = n // 2
-    pos = jnp.where(me % 2 == 0, me // 2, n - 1 - me // 2)
-
-    def at(position):
-        p = lax.rem(position + 2 * n, n)
-        return jnp.where(p < half, 2 * p, 2 * (n - 1 - p) + 1)
-
-    def slot_of(direction, hop):
-        return 0 if hop == 0 else n - 1 if hop == half else 2 * hop - 1 + direction
+    length = n // 2
+    z, y = me // 2, me % 2
+    partner = 2 * z + 1 - y
+    last = length - 1
+
+    def order(at, block):
+        gap = jnp.abs(at - block)
+        nearer = jnp.minimum(gap - 1, at) + jnp.minimum(gap - 1, last - at)
+        tied = jnp.where((block > at) & (gap <= at), 1, 0)
+        return 1 + nearer + tied
+
+    def held(r):
+        block = 0
+        for b in range(length):
+            block += jnp.where((order(z, b) == r) & (z != b), b, 0)
+        return block
+
+    blocks = [z] + [held(r) for r in range(1, length)]
+    onward = [None] + [jnp.where(b < z, z + 1, z - 1) for b in blocks[1:]]
 
     def rows_of(k, count=1):
         return pl.ds(k * rows, count * rows)
 
+    def cols_of(c):
+        return pl.ds(pl.multiple_of(c * width, width), width)
+
     barrier = pltpu.get_barrier_semaphore()
-    for sign in (-1, 1):
-        pl.semaphore_signal(
-            barrier, inc=1, device_id={"tensor": at(pos + sign)}, device_id_type=MESH
-        )
+
+    def greet(t):
+        pl.semaphore_signal(barrier, inc=1, device_id={"tensor": t}, device_id_type=MESH)
+
+    greet(partner)
+    pl.when(z > 0)(lambda: greet(me - 2))
+    pl.when(z < last)(lambda: greet(me + 2))
+
     own = pltpu.make_async_copy(hidden, hid_v, local_sem.at[0])
     own.start()
     scalars = []
@@ -262,146 +279,182 @@
         copy = pltpu.make_async_copy(src, dst, local_sem.at[1 + k])
         copy.start()
         scalars.append(copy)
-    weights = []
-    for c in range(chunks):
-        k = pl.ds(c * width, width)
-        pair = (
+
+    def weight_copies(c):
+        k = cols_of(c)
+        return (
             pltpu.make_async_copy(wq.at[k, :], wq_v.at[k, :], w_sem.at[0, c]),
             pltpu.make_async_copy(wkv.at[k, :], wkv_v.at[k, :], w_sem.at[1, c]),
         )
-        for copy in pair:
+
+    for c in range(chunks):
+        for copy in weight_copies(c):
             copy.start()
-        weights.append(pair)
     load_prompt = pltpu.make_async_copy(prompt, prompt_v, local_sem.at[4])
     load_prompt.start()
     load_pool = pltpu.make_async_copy(pool, pool_v, local_sem.at[5])
     load_pool.start()
 
-    def goes(direction, hop, c):
-        return hop < half or (hop == half and c % 2 == direction)
-
-    def ring_copy(direction, hop, c):
-        sign = 1 if direction == 0 else -1
-        cols = pl.ds(c * width, width)
-        send, recv = (right_send, right_recv) if direction == 0 else (left_send, left_recv)
+    def z_copy(r, c, dest, slot_there, send):
         return pltpu.make_async_remote_copy(
-            src_ref=gath.at[rows_of(slot_of(direction, hop - 1)), cols],
-            dst_ref=gath.at[rows_of(slot_of(direction, hop)), cols],
-            send_sem=send.at[hop - 1, c],
-            recv_sem=recv.at[hop - 1, c],
-            device_id={"tensor": at(pos + sign)},
+            src_ref=gath.at[rows_of(2 * r), cols_of(c)],
+            dst_ref=gath.at[rows_of(2 * slot_there), cols_of(c)],
+            send_sem=send,
+            recv_sem=z_recv.at[slot_there, c],
+            device_id={"tensor": 2 * dest + y},
             device_id_type=MESH,
         )
 
-    started = {}
-
-    def launch(hop, c):
-        for direction in (0, 1):
-            if goes(direction, hop, c):
-                copy = ring_copy(direction, hop, c)
-                copy.start()
-                started[direction, hop, c] = copy
-
-    def arrive(hop, c):
-        for direction in (0, 1):
-            if goes(direction, hop, c):
-                started[direction, hop, c].wait_recv()
-
-    def multiply(first, count, c):
-        if first == 0:
-            for copy in weights[c]:
-                copy.wait()
-        taken = slice(first * rows, (first + count) * rows)
-        x = gath[taken, c * width : (c + 1) * width]
-        for w, acc in ((wq_v, acc_q), (wkv_v, acc_kv)):
-            part = jnp.dot(x, w[c * width : (c + 1) * width, :], preferred_element_type=jnp.float32)
-            if c == 0:
-                acc[taken, :] = part
-            else:
-                acc[taken, :] += part
-
-    results = []
-
-    def hand_out(first, count):
-        taken = slice(first * rows, (first + count) * rows)
-        stage_q[taken, :] = acc_q[taken, :].astype(jnp.bfloat16)
-        stage_kv[taken, :] = acc_kv[taken, :].astype(jnp.bfloat16)
-        for k in range(max(first, 1), first + count):
-            hops = (k + 1) // 2
-            t = at(pos - hops if k % 2 == 1 else pos + hops)
-            for stage, out, cols, send, recv in (
-                (stage_q, q_out, q_cols, q_send, q_recv),
-                (stage_kv, kv_out, kv_cols, kv_send, kv_recv),
-            ):
-                copy = pltpu.make_async_remote_copy(
-                    src_ref=stage.at[rows_of(k), :],
-                    dst_ref=out.at[:, pl.ds(pl.multiple_of(me * cols, cols), cols)],
-                    send_sem=send.at[k],
-                    recv_sem=recv.at[k],
-                    device_id={"tensor": t},
-                    device_id_type=MESH,
-                )
-                copy.start()
-                results.append(copy)
-
+    def own_copy(side, c):
+        dest = z - 1 if side == 0 else z + 1
+        return z_copy(0, c, dest, order(dest, z), own_send.at[side, c])
+
+    def forward(r, c):
+        dest = onward[r]
+        return z_copy(r, c, dest, order(dest, blocks[r]), z_send.at[r, c])
+
+    def z_arrival(r, c):
+        return z_copy(r, c, jnp.where(z == 0, 1, z - 1), r, z_send.at[r, c])
+
+    def y_copy(r, c):
+        return pltpu.make_async_remote_copy(
+            src_ref=gath.at[rows_of(2 * r), cols_of(c)],
+            dst_ref=gath.at[rows_of(2 * r + 1), cols_of(c)],
+            send_sem=y_send.at[r, c],
+            recv_sem=y_recv.at[r, c],
+            device_id={"tensor": partner},
+            device_id_type=MESH,
+        )
+
+    def has_onward(r):
+        return (onward[r] >= 0) & (onward[r] <= last)
+
+    acc_q[...] = jnp.zeros_like(acc_q)
+    acc_kv[...] = jnp.zeros_like(acc_kv)
+    qbd[...] = jnp.zeros_like(qbd)
     own.wait()
     for c in range(chunks):
         cols = slice(c * width, (c + 1) * width)
         gath[rows_of(0), cols] = hid_v[:, :, cols].reshape(rows, width)
-    pl.semaphore_wait(barrier, 2)
+    pl.semaphore_wait(barrier, 1 + jnp.where(z > 0, 1, 0) + jnp.where(z < last, 1, 0))
+
     for c in range(chunks):
-        launch(1, c)
-    qbd[...] = jnp.zeros_like(qbd)
-    load_prompt.wait()
-    for hop in range(1, half - 1):
-        for c in range(chunks):
-            arrive(hop, c)
-            launch(hop + 1, c)
-    early = 2 * (half - 2) + 1
-    for c in range(chunks):
-        multiply(0, early, c)
-        arrive(half - 1, c)
-        launch(half, c)
-    hand_out(0, early)
-    for c in range(chunks):
-        arrive(half, c)
-        multiply(early, n - early, c)
-    hand_out(early, n - early)
-    prompts = []
-    for d in range(1, n):
-        t = lax.rem(me + d, n)
-        copy = pltpu.make_async_remote_copy(
+        pl.when(z > 0)(lambda c=c: own_copy(0, c).start())
+        pl.when(z < last)(lambda c=c: own_copy(1, c).start())
+        y_copy(0, c).start()
+
+    def phase(r):
+        first, count = (0, 3) if r == 0 else (2 * r + 1, 2 if r < last else 1)
+        taken = slice(first * rows, (first + count) * rows)
+
+        def step(c, carry):
+            if r < last:
+                z_arrival(r + 1, c).wait_recv()
+                pl.when(has_onward(r + 1))(lambda: forward(r + 1, c).start())
+                y_copy(r + 1, c).start()
+            y_copy(r, c).wait_recv()
+            if r == 0:
+                for copy in weight_copies(c):
+                    copy.wait()
+            x = gath[taken, cols_of(c)]
+            for w, acc in ((wq_v, acc_q), (wkv_v, acc_kv)):
+                acc[taken, :] += jnp.dot(x, w[cols_of(c), :], preferred_element_type=jnp.float32)
+            return carry
+
+        lax.fori_loop(0, chunks, step, 0)
+        stage_q[taken, :] = acc_q[taken, :].astype(jnp.bfloat16)
+        stage_kv[taken, :] = acc_kv[taken, :].astype(jnp.bfloat16)
+
+    sends = []
+
+    def hand_out(k):
+        t = 2 * blocks[k // 2] + (y if k % 2 == 0 else 1 - y)
+        for stage, out, cols, send, recv in (
+            (stage_q, q_out, q_cols, q_send, q_recv),
+            (stage_kv, kv_out, kv_cols, kv_send, kv_recv),
+        ):
+            copy = pltpu.make_async_remote_copy(
+                src_ref=stage.at[rows_of(k), :],
+                dst_ref=out.at[:, pl.ds(pl.multiple_of(me * cols, cols), cols)],
+                send_sem=send.at[k],
+                recv_sem=recv.at[me],
+                device_id={"tensor": t},
+                device_id_type=MESH,
+            )
+            copy.start()
+            sends.append(copy)
+
+    def prompt_copy(k):
+        t = 2 * blocks[k // 2] + (y if k % 2 == 0 else 1 - y)
+        return pltpu.make_async_remote_copy(
             src_ref=prompt_v.at[t],
             dst_ref=prompt_out.at[:, pl.ds(pl.multiple_of(me * kv_cols, kv_cols), kv_cols)],
-            send_sem=p_send.at[d],
-            recv_sem=p_recv.at[d],
+            send_sem=p_send.at[k],
+            recv_sem=p_recv.at[me],
             device_id={"tensor": t},
             device_id_type=MESH,
         )
-        prompts.append(copy)
-    for copy in prompts:
+
+    for r in range(length):
+        phase(r)
+        if r < last:
+            hand_out(2 * r + 2)
+        if r == last - 1:
+            load_prompt.wait()
+            for k in range(1, n - 1, 2):
+                hand_out(k)
+            for k in range(2, n, 2):
+                copy = prompt_copy(k)
+                copy.start()
+                sends.append(copy)
+    hand_out(n - 1)
+    for k in range(1, n, 2):
+        copy = prompt_copy(k)
         copy.start()
+        sends.append(copy)
+
     for source, out, cols in (
         (stage_q[0:rows, :], q_out, q_cols),
         (stage_kv[0:rows, :], kv_out, kv_cols),
         (prompt_v[me], prompt_out, kv_cols),
     ):
         out[:, pl.ds(pl.multiple_of(me * cols, cols), cols)] = source
-    for copy in results:
-        copy.wait()
+
+    def arrival(out, cols, recv, d):
+        t = lax.rem(me + d, n)
+        here = out.at[:, pl.ds(pl.multiple_of(t * cols, cols), cols)]
+        return pltpu.make_async_remote_copy(
+            src_ref=here, dst_ref=here, send_sem=recv.at[t], recv_sem=recv.at[t],
+            device_id={"tensor": t}, device_id_type=MESH,
+        )
+
+    for d in range(1, n):
+        arrival(q_out, q_cols, q_recv, d).wait_recv()
+        arrival(kv_out, kv_cols, kv_recv, d).wait_recv()
     for copy in scalars:
         copy.wait()
     load_pool.wait()
 
     def after():
-        for copy in prompts:
-            copy.wait()
+        for d in range(1, n):
+            arrival(prompt_out, kv_cols, p_recv, d).wait_recv()
 
     attend_resident(
         table, lens, slot, pool_v, q_out, kv_out, prompt_out, qbd, op, attended, after
     )
-    for copy in started.values():
+    for copy in sends:
         copy.wait_send()
+
+    def drain(c, carry):
+        pl.when(z > 0)(lambda: own_copy(0, c).wait_send())
+        pl.when(z < last)(lambda: own_copy(1, c).wait_send())
+        for r in range(length):
+            y_copy(r, c).wait_send()
+            if r > 0:
+                pl.when(has_onward(r))(lambda r=r: forward(r, c).wait_send())
+        return carry
+
+    lax.fori_loop(0, chunks, drain, 0)
 
 
 def relay(hidden, wq, wkv, prompt, pool, table, lens, slot, n):
@@ -439,6 +492,7 @@
             pltpu.VMEM((n * rows, kv_cols), jnp.float32),
             pltpu.VMEM((n * rows, q_cols), jnp.bfloat16),
             pltpu.VMEM((n * rows, kv_cols), jnp.bfloat16),
+            dma((2, chunks)),
             dma((half, chunks)),
             dma((half, chunks)),
             dma((half, chunks)),

time: 55 us -> 54.7 us (level)
  no operation moved by 1% of the time
where the time goes in v2:
time: 54.7 us; the launch traced here: 54.5 us
  Pallas kernels  52 us (95%)
  local copies, waits for them, and re-layouts  1.83 us (3%)
  between operations  0.66 us (1%)
    pallas_call x1, Pallas kernels, relay(): pl.pallas_call(functools.partial(relay_kernel, n, chunks), out_shape=jax....  52 us
    reshape x1, local copies, waits for them, and re-layouts, per_device(): return out.reshape(seqs, 2, out.shape[1])  1.83 us

profile of v2, /device:TPU:0, one launch (start us, length us, event | category | flops | bytes accessed | tf_op | source)
XLA Modules:
  0.0 54.5 jit_solution(14388642845388396288)
XLA Ops:
  0.7 52.0 %relay.1 = bf16[16,8192]{1,0:T(8,128)(2,1)} custom-call(s32[2,8]{1,0:T(2,128)} %bitcast.1, s32[8]{0:T(128)} %lens_h.1, s32[1]{0:T(128)S(6)} %copy.9.slot_h, bf16[8,2,8192]{2,1,0:T(2,128)(2,1)} %hidden.1, bf16[8192,1024]{1,0:T(8,128)(2,1)} %wq.1, bf16[8192,256]{1,0:T(8,128)(2,1)} %wkv.1, bf16[8,128,256]{2,1,0:T(8,128)(2,1)} %prompt.1, bf16[16,128,2048]{2,1,0:T(8,128)(2,1)} %pool.1), custom_call_target="tpu_custom_call" | custom-call | tf_op jit(solution)/shard_map/relay/pallas_call | solution.py:471
  52.7 1.8 %reshape.3 = bf16[8,2,8192]{2,1,0:T(2,128)(2,1)} reshape(bf16[16,8192]{1,0:T(8,128)(2,1)} %relay.1) | data formatting | bytes 524288 | tf_op jit(solution)/shard_map/reshape | solution.py:535

commit v3 on v2

--- a/solution.py
+++ b/solution.py
@@ -245,14 +245,30 @@
     def order(at, block):
         gap = jnp.abs(at - block)
         nearer = jnp.minimum(gap - 1, at) + jnp.minimum(gap - 1, last - at)
-        tied = jnp.where((block > at) & (gap <= at), 1, 0)
-        return 1 + nearer + tied
+        both = (gap <= at) & (gap <= last - at)
+        favoured = (block > at) == (at % 2 == 0)
+        return 1 + nearer + jnp.where(both & jnp.logical_not(favoured), 1, 0)
 
     def held(r):
         block = 0
         for b in range(length):
             block += jnp.where((order(z, b) == r) & (z != b), b, 0)
         return block
+
+    groups = [[(0, 0), (1, 0), (0, 1), (0, 2)]]
+    groups[0] += [(1, 1)]
+    groups += [[(1, r), (0, r + 1)] for r in range(2, last)]
+    groups += [[(1, last)]]
+    seats = [seat for group in groups for seat in group]
+    place = {seat: k for k, seat in enumerate(seats)}
+    z_place = [place[0, r] for r in range(length)]
+    y_place = [place[1, r] for r in range(length)]
+
+    def place_there(slot_there):
+        found = 0
+        for r in range(1, length):
+            found += jnp.where(slot_there == r, z_place[r], 0)
+        return found
 
     blocks = [z] + [held(r) for r in range(1, length)]
     onward = [None] + [jnp.where(b < z, z + 1, z - 1) for b in blocks[1:]]
@@ -280,25 +296,19 @@
         copy.start()
         scalars.append(copy)
 
-    def weight_copies(c):
-        k = cols_of(c)
-        return (
-            pltpu.make_async_copy(wq.at[k, :], wq_v.at[k, :], w_sem.at[0, c]),
-            pltpu.make_async_copy(wkv.at[k, :], wkv_v.at[k, :], w_sem.at[1, c]),
-        )
-
-    for c in range(chunks):
-        for copy in weight_copies(c):
-            copy.start()
+    weights = (
+        pltpu.make_async_copy(wq, wq_v, w_sem.at[0]),
+        pltpu.make_async_copy(wkv, wkv_v, w_sem.at[1]),
+    )
+    for copy in weights:
+        copy.start()
     load_prompt = pltpu.make_async_copy(prompt, prompt_v, local_sem.at[4])
-    load_prompt.start()
     load_pool = pltpu.make_async_copy(pool, pool_v, local_sem.at[5])
-    load_pool.start()
 
     def z_copy(r, c, dest, slot_there, send):
         return pltpu.make_async_remote_copy(
-            src_ref=gath.at[rows_of(2 * r), cols_of(c)],
-            dst_ref=gath.at[rows_of(2 * slot_there), cols_of(c)],
+            src_ref=gath.at[rows_of(z_place[r]), cols_of(c)],
+            dst_ref=gath.at[rows_of(place_there(slot_there)), cols_of(c)],
             send_sem=send,
             recv_sem=z_recv.at[slot_there, c],
             device_id={"tensor": 2 * dest + y},
@@ -318,8 +328,8 @@
 
     def y_copy(r, c):
         return pltpu.make_async_remote_copy(
-            src_ref=gath.at[rows_of(2 * r), cols_of(c)],
-            dst_ref=gath.at[rows_of(2 * r + 1), cols_of(c)],
+            src_ref=gath.at[rows_of(z_place[r]), cols_of(c)],
+            dst_ref=gath.at[rows_of(y_place[r]), cols_of(c)],
             send_sem=y_send.at[r, c],
             recv_sem=y_recv.at[r, c],
             device_id={"tensor": partner},
@@ -344,8 +354,14 @@
         y_copy(0, c).start()
 
     def phase(r):
-        first, count = (0, 3) if r == 0 else (2 * r + 1, 2 if r < last else 1)
-        taken = slice(first * rows, (first + count) * rows)
+        if r == 1:
+            for copy in weights:
+                copy.wait()
+            load_prompt.start()
+            load_pool.start()
+        group = groups[max(r - 1, 0)]
+        first = place[group[0]]
+        taken = slice(first * rows, (first + len(group)) * rows)
 
         def step(c, carry):
             if r < last:
@@ -354,21 +370,24 @@
                 y_copy(r + 1, c).start()
             y_copy(r, c).wait_recv()
             if r == 0:
-                for copy in weight_copies(c):
-                    copy.wait()
+                return carry
             x = gath[taken, cols_of(c)]
             for w, acc in ((wq_v, acc_q), (wkv_v, acc_kv)):
                 acc[taken, :] += jnp.dot(x, w[cols_of(c), :], preferred_element_type=jnp.float32)
             return carry
 
         lax.fori_loop(0, chunks, step, 0)
-        stage_q[taken, :] = acc_q[taken, :].astype(jnp.bfloat16)
-        stage_kv[taken, :] = acc_kv[taken, :].astype(jnp.bfloat16)
+        if r > 0:
+            stage_q[taken, :] = acc_q[taken, :].astype(jnp.bfloat16)
+            stage_kv[taken, :] = acc_kv[taken, :].astype(jnp.bfloat16)
 
     sends = []
 
-    def hand_out(k):
-        t = 2 * blocks[k // 2] + (y if k % 2 == 0 else 1 - y)
+    def owner(seat):
+        return 2 * blocks[seat[1]] + (y if seat[0] == 0 else 1 - y)
+
+    def hand_out(seat):
+        k, t = place[seat], owner(seat)
         for stage, out, cols, send, recv in (
             (stage_q, q_out, q_cols, q_send, q_recv),
             (stage_kv, kv_out, kv_cols, kv_send, kv_recv),
@@ -384,9 +403,9 @@
             copy.start()
             sends.append(copy)
 
-    def prompt_copy(k):
-        t = 2 * blocks[k // 2] + (y if k % 2 == 0 else 1 - y)
-        return pltpu.make_async_remote_copy(
+    def send_prompt(seat):
+        k, t = place[seat], owner(seat)
+        copy = pltpu.make_async_remote_copy(
             src_ref=prompt_v.at[t],
             dst_ref=prompt_out.at[:, pl.ds(pl.multiple_of(me * kv_cols, kv_cols), kv_cols)],
             send_sem=p_send.at[k],
@@ -394,24 +413,24 @@
             device_id={"tensor": t},
             device_id_type=MESH,
         )
+        copy.start()
+        sends.append(copy)
 
     for r in range(length):
         phase(r)
         if r < last:
-            hand_out(2 * r + 2)
+            for seat in groups[r - 1] if r > 0 else []:
+                if seat[0] == 0 and seat[1] > 0:
+                    hand_out(seat)
         if r == last - 1:
             load_prompt.wait()
-            for k in range(1, n - 1, 2):
-                hand_out(k)
-            for k in range(2, n, 2):
-                copy = prompt_copy(k)
-                copy.start()
-                sends.append(copy)
-    hand_out(n - 1)
-    for k in range(1, n, 2):
-        copy = prompt_copy(k)
-        copy.start()
-        sends.append(copy)
+            for q in range(0, last):
+                hand_out((1, q))
+            for q in range(1, length):
+                send_prompt((0, q))
+    hand_out((1, last))
+    for q in range(length):
+        send_prompt((1, q))
 
     for source, out, cols in (
         (stage_q[0:rows, :], q_out, q_cols),
@@ -503,7 +522,7 @@
             dma((n,)),
             dma((n,)),
             dma((n,)),
-            dma((2, chunks)),
+            dma((2,)),
             dma((6,)),
         ],
         compiler_params=pltpu.CompilerParams(
@@ -527,7 +546,7 @@
     seqs = hidden.shape[0]
     flat = hidden.reshape(seqs * 2, hidden.shape[2])
     aligned = wq.shape[1] % 128 == 0 and wkv.shape[1] % 128 == 0
-    if aligned and n % 2 == 0 and n > 4 and flat.shape[0] % 16 == 0 and prompt_kv.shape[0] == n:
+    if aligned and n % 4 == 0 and n > 4 and flat.shape[0] % 16 == 0 and prompt_kv.shape[0] == n:
         out = relay(hidden, wq, wkv, prompt_kv, cache_pool, page_table, ctx_len, prompt_slot, n)
     else:
         query, keyval, prompt = exchange(flat, wq, wkv, prompt_kv)

time: 54.7 us -> 51.6 us (0.943)
  Pallas kernels: 52 us -> 49 us
    pallas_call x1, Pallas kernels: 52 us -> 49 us  [relay(): pl.pallas_call(functools.partial(relay_kernel, n, chunks), out_shape=jax....]
where the time goes in v3:
time: 51.6 us; the launch traced here: 51.5 us
  Pallas kernels  49 us (95%)
  local copies, waits for them, and re-layouts  1.83 us (4%)
  between operations  0.66 us (1%)
    pallas_call x1, Pallas kernels, relay(): pl.pallas_call(functools.partial(relay_kernel, n, chunks), out_shape=jax....  49 us
    reshape x1, local copies, waits for them, and re-layouts, per_device(): return out.reshape(seqs, 2, out.shape[1])  1.83 us

profile of v3, /device:TPU:0, one launch (start us, length us, event | category | flops | bytes accessed | tf_op | source)
XLA Modules:
  0.0 51.5 jit_solution(11457297883137559619)
XLA Ops:
  0.7 49.0 %relay.1 = bf16[16,8192]{1,0:T(8,128)(2,1)} custom-call(s32[2,8]{1,0:T(2,128)} %bitcast.1, s32[8]{0:T(128)} %lens_h.1, s32[1]{0:T(128)S(6)} %copy.9.slot_h, bf16[8,2,8192]{2,1,0:T(2,128)(2,1)} %hidden.1, bf16[8192,1024]{1,0:T(8,128)(2,1)} %wq.1, bf16[8192,256]{1,0:T(8,128)(2,1)} %wkv.1, bf16[8,128,256]{2,1,0:T(8,128)(2,1)} %prompt.1, bf16[16,128,2048]{2,1,0:T(8,128)(2,1)} %pool.1), custom_call_target="tpu_custom_call" | custom-call | tf_op jit(solution)/shard_map/relay/pallas_call | solution.py:490
  49.7 1.8 %reshape.3 = bf16[8,2,8192]{2,1,0:T(2,128)(2,1)} reshape(bf16[16,8192]{1,0:T(8,128)(2,1)} %relay.1) | data formatting | bytes 524288 | tf_op jit(solution)/shard_map/reshape | solution.py:554

commit v4 on v3

--- a/solution.py
+++ b/solution.py
@@ -13,7 +13,6 @@
 GROUP = QUERY_HEADS // KEY_VALUE_HEADS
 MESH = pl.DeviceIdType.MESH
 NEG = -1e30
-UNROLL = 2
 
 
 def dot_t(a, b):
@@ -138,7 +137,10 @@
     )(table.reshape(-1), lens, slot, *([pool] * pages), query, keyval, prompt)
 
 
-def attend_resident(table, lens, slot, pool_v, q_out, kv_out, prompt_out, qbd, op, out, after):
+def attend_resident(
+    table, lens, slot, pool_v, q_out, kv_out, prompt_out, qbd, ubd, qh, held, stat, op, out,
+    parity, first_half, second_half, after,
+):
     seqs = lens.shape[0]
     pages = table.shape[0]
     rows = seqs * 2
@@ -156,19 +158,36 @@
         source = (rest % GROUP) * rows + seq * 2 + rest // GROUP
         return jnp.where(c == source, 1.0, 0.0).astype(jnp.bfloat16)
 
-    p = perm(False)
-    for h in range(KEY_VALUE_HEADS):
-        tiles = [
-            q_out[:, (h * GROUP + g) * HEAD_SIZE : (h * GROUP + g + 1) * HEAD_SIZE]
-            for g in range(GROUP)
-        ]
-        ordered = jnp.dot(
-            p, jnp.concatenate(tiles, axis=0), preferred_element_type=jnp.float32
-        ).astype(jnp.bfloat16)
-        for s in range(seqs):
-            qbd[s, h * block : (h + 1) * block, h * HEAD_SIZE : (h + 1) * HEAD_SIZE] = ordered[
-                s * block : (s + 1) * block, :
+    pairs = seqs // 2
+    side = KEY_VALUE_HEADS // 2
+
+    def head(e, par):
+        return 2 * (e % side) + par
+
+    def head_cols(e, par, base=0):
+        return pl.ds(pl.multiple_of(base + head(e, par) * HEAD_SIZE, HEAD_SIZE), HEAD_SIZE)
+
+    def spread_queries(half, par):
+        p = perm(False)
+        for e in range(side):
+            h = head(e, par)
+            tiles = [
+                q_out[:, pl.ds(pl.multiple_of((h * GROUP + g) * HEAD_SIZE, HEAD_SIZE), HEAD_SIZE)]
+                for g in range(GROUP)
             ]
+            ordered = jnp.dot(
+                p, jnp.concatenate(tiles, axis=0), preferred_element_type=jnp.float32
+            ).astype(jnp.bfloat16)
+            qh[h] = ordered
+            for s in range(seqs):
+                piece = ordered[s * block : (s + 1) * block, :]
+                qbd[s, pl.ds(pl.multiple_of(h * block, block), block), head_cols(e, par)] = piece
+                k = s % 2 * side + e
+                ubd[
+                    half * pairs + s // 2,
+                    k * block : (k + 1) * block,
+                    k * HEAD_SIZE : (k + 1) * HEAD_SIZE,
+                ] = piece
 
     key = lax.broadcasted_iota(jnp.int32, (page_rows, lanes), 0)
     new_key = lax.broadcasted_iota(jnp.int32, (rows, lanes), 0)
@@ -202,14 +221,76 @@
             outs.append(acc.astype(jnp.bfloat16))
         return outs
 
-    def several(k, carry):
-        for u in range(UNROLL):
-            s = k * UNROLL + u
-            for h, o in enumerate(one(s, False)):
-                op[h, pl.ds(pl.multiple_of(s * block, block), block), :] = o
-        return carry
-
-    lax.fori_loop(0, seqs // UNROLL, several, 0)
+    lane_seq = lax.broadcasted_iota(jnp.int32, (1, lanes), 1) // (side * block)
+
+    def cache_part(half, k, par):
+        q = ubd[half * pairs + k]
+        spots = [[table[p, 2 * k + u] for u in range(2)] for p in range(pages)]
+        limit = jnp.where(lane_seq == 0, lens[2 * k], lens[2 * k + 1])
+        parts = []
+        for p in range(pages):
+            keys = [pool_v[spots[p][e // side], :, head_cols(e, par)] for e in range(2 * side)]
+            sc = dot_t(jnp.concatenate(keys, axis=1), q) * scale
+            parts.append(jnp.where(key + p * page_rows < limit, sc, NEG))
+        top = functools.reduce(jnp.maximum, [jnp.max(x, axis=0, keepdims=True) for x in parts])
+        expo = [jnp.exp(x - top) for x in parts]
+        norm = functools.reduce(jnp.add, [jnp.sum(e, axis=0, keepdims=True) for e in expo])
+        wide = jnp.concatenate([jnp.transpose(e).astype(jnp.bfloat16) for e in expo], axis=1)
+        tops = jnp.transpose(jnp.broadcast_to(top, (8, lanes)))
+        norms = jnp.transpose(jnp.broadcast_to(norm, (8, lanes)))
+        for e in range(2 * side):
+            v = jnp.concatenate(
+                [pool_v[spots[p][e // side], :, head_cols(e, par, kv_half)] for p in range(pages)],
+                axis=0,
+            )
+            mine = slice(e * block, (e + 1) * block)
+            there = pl.ds(pl.multiple_of((2 * k + e // side) * block, block), block)
+            stat[head(e, par), there, 0:8] = tops[mine]
+            stat[head(e, par), there, 8:16] = norms[mine]
+            held[head(e, par), there, :] = jnp.dot(wide[mine], v, preferred_element_type=jnp.float32)
+
+    def merge():
+        row = lax.broadcasted_iota(jnp.int32, (total, rows), 0)
+        col = lax.broadcasted_iota(jnp.int32, (total, rows), 1)
+        live = (col // 2 == row // block) & (col % 2 <= row // GROUP % 2)
+        heads = range(KEY_VALUE_HEADS)
+        scores = [
+            dot_t(qh[h], kv_out[:, h * HEAD_SIZE : (h + 1) * HEAD_SIZE]) * scale for h in heads
+        ]
+        scores = [jnp.where(live, sc, NEG) for sc in scores]
+        tops = [
+            jnp.maximum(stat[h, :, 0:1], jnp.max(scores[h], axis=1, keepdims=True)) for h in heads
+        ]
+        shrinks = [jnp.exp(stat[h, :, 0:1] - tops[h]) for h in heads]
+        expos = [jnp.exp(scores[h] - tops[h]) for h in heads]
+        norms = [
+            shrinks[h] * stat[h, :, 8:9] + jnp.sum(expos[h], axis=1, keepdims=True) for h in heads
+        ]
+        fresh = [
+            jnp.dot(
+                (expos[h] / norms[h]).astype(jnp.bfloat16),
+                kv_out[:, kv_half + h * HEAD_SIZE : kv_half + (h + 1) * HEAD_SIZE],
+                preferred_element_type=jnp.float32,
+            )
+            for h in heads
+        ]
+        for h in heads:
+            op[h] = (held[h] * (shrinks[h] / norms[h]) + fresh[h]).astype(jnp.bfloat16)
+
+    def sweep(part, half, par):
+        def step(k, carry):
+            part(half, k, par)
+            return carry
+
+        lax.fori_loop(0, pairs, step, 0, unroll=4)
+
+    first_half()
+    spread_queries(0, parity)
+    sweep(cache_part, 0, parity)
+    second_half()
+    spread_queries(1, 1 - parity)
+    sweep(cache_part, 1, 1 - parity)
+    merge()
     after()
     chosen = slot[0]
     continued = one(chosen, True)
@@ -228,7 +309,7 @@
 def relay_kernel(
     n, chunks, table_h, lens_h, slot_h, hidden, wq, wkv, prompt, pool, attended,
     table, lens, slot, hid_v,
-    q_out, kv_out, prompt_out, prompt_v, pool_v, qbd, op,
+    q_out, kv_out, prompt_out, prompt_v, pool_v, qbd, ubd, qh, held_acc, stat, op,
     gath, wq_v, wkv_v, acc_q, acc_kv, stage_q, stage_kv,
     own_send, z_send, z_recv, y_send, y_recv,
     q_send, q_recv, kv_send, kv_recv, p_send, p_recv, w_sem, local_sem,
@@ -342,6 +423,7 @@
     acc_q[...] = jnp.zeros_like(acc_q)
     acc_kv[...] = jnp.zeros_like(acc_kv)
     qbd[...] = jnp.zeros_like(qbd)
+    ubd[...] = jnp.zeros_like(ubd)
     own.wait()
     for c in range(chunks):
         cols = slice(c * width, (c + 1) * width)
@@ -447,19 +529,27 @@
             device_id={"tensor": t}, device_id_type=MESH,
         )
 
-    for d in range(1, n):
-        arrival(q_out, q_cols, q_recv, d).wait_recv()
-        arrival(kv_out, kv_cols, kv_recv, d).wait_recv()
     for copy in scalars:
         copy.wait()
     load_pool.wait()
 
+    def first_half():
+        for d in range(2, n, 2):
+            arrival(q_out, q_cols, q_recv, d).wait_recv()
+
+    def second_half():
+        for d in range(1, n):
+            if d % 2 == 1:
+                arrival(q_out, q_cols, q_recv, d).wait_recv()
+            arrival(kv_out, kv_cols, kv_recv, d).wait_recv()
+
     def after():
         for d in range(1, n):
             arrival(prompt_out, kv_cols, p_recv, d).wait_recv()
 
     attend_resident(
-        table, lens, slot, pool_v, q_out, kv_out, prompt_out, qbd, op, attended, after
+        table, lens, slot, pool_v, q_out, kv_out, prompt_out, qbd, ubd, qh, held_acc, stat, op,
+        attended, y, first_half, second_half, after,
     )
     for copy in sends:
         copy.wait_send()
@@ -503,6 +593,10 @@
             pltpu.VMEM(prompt.shape, jnp.bfloat16),
             pltpu.VMEM(pool.shape, jnp.bfloat16),
             pltpu.VMEM((seqs, KEY_VALUE_HEADS * 2 * GROUP, KEY_VALUE_HEADS * HEAD_SIZE), jnp.bfloat16),
+            pltpu.VMEM((seqs, KEY_VALUE_HEADS * 2 * GROUP, KEY_VALUE_HEADS * HEAD_SIZE), jnp.bfloat16),
+            pltpu.VMEM((KEY_VALUE_HEADS, rows * GROUP, HEAD_SIZE), jnp.bfloat16),
+            pltpu.VMEM((KEY_VALUE_HEADS, rows * GROUP, HEAD_SIZE), jnp.float32),
+            pltpu.VMEM((KEY_VALUE_HEADS, rows * GROUP, 16), jnp.float32),
             pltpu.VMEM((KEY_VALUE_HEADS, rows * GROUP, HEAD_SIZE), jnp.bfloat16),
             pltpu.VMEM((n * rows, depth), jnp.bfloat16),
             pltpu.VMEM((depth, q_cols), jnp.bfloat16),
@@ -546,7 +640,7 @@
     seqs = hidden.shape[0]
     flat = hidden.reshape(seqs * 2, hidden.shape[2])
     aligned = wq.shape[1] % 128 == 0 and wkv.shape[1] % 128 == 0
-    if aligned and n % 4 == 0 and n > 4 and flat.shape[0] % 16 == 0 and prompt_kv.shape[0] == n:
+    if aligned and n == KEY_VALUE_HEADS and flat.shape[0] % 16 == 0 and prompt_kv.shape[0] == n:
         out = relay(hidden, wq, wkv, prompt_kv, cache_pool, page_table, ctx_len, prompt_slot, n)
     else:
         query, keyval, prompt = exchange(flat, wq, wkv, prompt_kv)

time: 51.6 us -> 49.3 us (0.955)
  Pallas kernels: 49 us -> 46.7 us
    pallas_call x1, Pallas kernels: 49 us -> 46.7 us  [relay(): pl.pallas_call(functools.partial(relay_kernel, n, chunks), out_shape=jax....]
where the time goes in v4:
time: 49.3 us; the launch traced here: 49.2 us
  Pallas kernels  46.7 us (95%)
  local copies, waits for them, and re-layouts  1.83 us (4%)
  between operations  0.66 us (1%)
    pallas_call x1, Pallas kernels, relay(): pl.pallas_call(functools.partial(relay_kernel, n, chunks), out_shape=jax....  46.7 us
    reshape x1, local copies, waits for them, and re-layouts, per_device(): return out.reshape(seqs, 2, out.shape[1])  1.83 us

profile of v4, /device:TPU:0, one launch (start us, length us, event | category | flops | bytes accessed | tf_op | source)
XLA Modules:
  0.0 49.2 jit_solution(3486486039816801850)
XLA Ops:
  0.7 46.7 %relay.1 = bf16[16,8192]{1,0:T(8,128)(2,1)} custom-call(s32[2,8]{1,0:T(2,128)} %bitcast.1, s32[8]{0:T(128)} %lens_h.1, s32[1]{0:T(128)S(6)} %copy.9.slot_h, bf16[8,2,8192]{2,1,0:T(2,128)(2,1)} %hidden.1, bf16[8192,1024]{1,0:T(8,128)(2,1)} %wq.1, bf16[8192,256]{1,0:T(8,128)(2,1)} %wkv.1, bf16[8,128,256]{2,1,0:T(8,128)(2,1)} %prompt.1, bf16[16,128,2048]{2,1,0:T(8,128)(2,1)} %pool.1), custom_call_target="tpu_custom_call" | custom-call | tf_op jit(solution)/shard_map/relay/pallas_call | solution.py:580
  47.3 1.8 %reshape.3 = bf16[8,2,8192]{2,1,0:T(2,128)(2,1)} reshape(bf16[16,8192]{1,0:T(8,128)(2,1)} %relay.1) | data formatting | bytes 524288 | tf_op jit(solution)/shard_map/reshape | solution.py:648
